TPU v7x, 16 devices: a 4x2x1 block of a 4x4x8 slice. The times are simulated.
16 devices in a mesh: replica: 2 (over y, z), data: 8 (over x, core).
Axes of the slice: x: 4, y: 2, z: 1, core: 2. Of those that a mesh axis runs over, the one named last changes fastest.
The devices are a block of a 4x4x8 slice.
Arguments:
- q_hidden: bfloat16 [256, 32, 1024], P(('replica', 'data')), parts along dimension 0
- d_hidden: bfloat16 [256, 512, 1024], P(('replica', 'data')), parts along dimension 0
- w_proj: bfloat16 [1024, 128], replicated
- q_mask: int32 [256, 32], P(('replica', 'data')), parts along dimension 0
- d_mask: int32 [256, 512], P(('replica', 'data')), parts along dimension 0
- temperature: float32 [], replicated
Outputs:
- output 1: float32 [256], P(('replica', 'data')), parts along dimension 0
- output 2: float32 [256], P(('replica', 'data')), parts along dimension 0
- output 3: float32 [2], P('replica'), parts along dimension 0
There are 2 independent parts. A program takes and returns all parts, laid end to end along the dimension named above; an argument that names none is the same for every part.
All inputs are finite; a program needn't handle non-finite values.
Results may differ from a plain program's by a relative error of at most 0.001.
Values are sent between devices in bfloat16 or wider.
A program may use at most 768 MiB of HBM per device.

v0:
```python
import functools
import jax
import jax.numpy as jnp
from jax import lax
from jax.sharding import PartitionSpec as P

TILE_ELEMS = 8388608


def project(hidden, w_proj):
    raw_proj = jnp.einsum('bth,hk->btk', hidden, w_proj, preferred_element_type=jnp.float32)
    return (raw_proj / jnp.sqrt(jnp.sum(raw_proj * raw_proj, axis=-1, keepdims=True))).astype(jnp.bfloat16)


def blocks_per_step(total_blocks, block_elems):
    chosen = 1
    for candidate in range(1, total_blocks + 1):
        if total_blocks % candidate == 0 and candidate * block_elems <= TILE_ELEMS:
            chosen = candidate
    return chosen


def maxsim(q_vecs, p_vecs, d_mask):
    sim_vals = jnp.einsum('itk,jsk->itjs', q_vecs, p_vecs, preferred_element_type=jnp.float32)
    best_sim = jnp.max(jnp.where(d_mask[None, None, :, :] == 1, sim_vals, -jnp.inf), axis=3)
    return jnp.sum(best_sim, axis=1)


def solution(mesh):
    group_size = mesh.shape['data']
    batch_spec = P(('replica', 'data'))

    def local_loss(q_hidden, d_hidden, w_proj, q_mask, d_mask, value_a11):
        local_pairs = q_hidden.shape[0]
        q_len = q_hidden.shape[1]
        d_len = d_hidden.shape[1]
        proj_dim = w_proj.shape[1]
        q_vecs = jnp.where(q_mask[:, :, None] == 1, project(q_hidden, w_proj), 0.0).astype(jnp.bfloat16)
        p_vecs = project(d_hidden, w_proj)
        q_group = lax.all_gather(q_vecs, 'data', tiled=True)
        step_blocks = blocks_per_step(group_size, local_pairs * local_pairs * q_len * d_len)
        q_steps = q_group.reshape(group_size // step_blocks, step_blocks * local_pairs, q_len, proj_dim)
        col_scores = lax.map(functools.partial(maxsim, p_vecs=p_vecs, d_mask=d_mask), q_steps)
        col_scores = col_scores.reshape(group_size * local_pairs, local_pairs)
        row_scores = lax.all_to_all(col_scores, 'data', 0, 1, tiled=True)
        my_index = lax.axis_index('data')
        own_block = lax.dynamic_slice_in_dim(col_scores, my_index * local_pairs, local_pairs, axis=0)
        pos_logit = jnp.diagonal(own_block) / value_a11
        loss_query = jax.nn.logsumexp(row_scores / value_a11, axis=1) - pos_logit
        loss_doc = jax.nn.logsumexp(col_scores / value_a11, axis=0) - pos_logit
        group_sum = lax.psum(jnp.sum(loss_query + loss_doc), 'data')
        loss_mean = (group_sum / (2 * group_size * local_pairs)).reshape(1)
        return loss_query, loss_doc, loss_mean

    return jax.shard_map(local_loss, mesh=mesh, in_specs=(batch_spec, batch_spec, P(), batch_spec, batch_spec, P()), out_specs=(batch_spec, batch_spec, P('replica')), check_vma=False)
```

profile of v0, /device:TPU:113, one launch (start us, length us, event | category | flops | bytes accessed | tf_op | source)
XLA Modules:
  0.0 93.1 jit_solution(16186672065663031687)
XLA Ops:
  7.3 1.1 %copy-done = bf16[16,32,1024]{2,1,0:T(8,128)(2,1)S(1)} copy-done((bf16[16,32,1024]{2,1,0:T(8,128)(2,1)S(1)}, bf16[16,32,1024]{2,1,0:T(8,128)(2,1)}, u32[]{:S(2)}) %copy-start) | copy-done | bytes 1048600
  8.4 1.5 %multiply_reduce_fusion.1 = (f32[16,32]{1,0:T(8,128)S(1)}, f32[16,32,128]{2,1,0:T(8,128)S(1)}) fusion(bf16[16,32,1024]{2,1,0:T(8,128)(2,1)S(1)} %copy-done, bf16[1024,128]{1,0:T(8,128)(2,1)} %param.10), kind=kOutput, calls=%fused_computation.15 | convolution fusion | flops 134348288 | bytes 1574912 | tf_op jit(solution)/shard_map/bth,hk->btk/dot_general | solution.py:11
  9.9 0.7 broadcast_compare_fusion.1
  10.6 0.8 fusion.8
  11.5 13.3 %multiply_reduce_fusion = (f32[16,512]{1,0:T(8,128)S(1)}, f32[16,512,128]{1,2,0:T(8,128)}) fusion(bf16[16,512,1024]{2,1,0:T(8,128)(2,1)} %param.9, bf16[1024,128]{1,0:T(8,128)(2,1)} %param.10), kind=kOutput, calls=%fused_computation.9 | convolution fusion | flops 2149572608 | bytes 21266432 | tf_op jit(solution)/shard_map/bth,hk->btk/dot_general | solution.py:11
  24.8 2.8 %divide_convert_fusion = bf16[16,512,128]{1,2,0:T(8,128)(2,1)S(1)} fusion(f32[16,512,128]{1,2,0:T(8,128)} %get-tuple-element.67, f32[16,512]{1,0:T(8,128)S(1)} %sqrt.17), kind=kLoop, calls=%fused_computation.8 | loop fusion | flops 2097152 | bytes 6324224 | tf_op jit(solution)/shard_map/convert_element_type | solution.py:12
  27.6 2.4 %copy.23 = bf16[16,512,128]{2,1,0:T(8,128)(2,1)} copy(bf16[16,512,128]{1,2,0:T(8,128)(2,1)S(1)} %divide_convert_fusion) | data formatting | bytes 4194304 | tf_op jit(solution)/shard_map/while | solution.py:43
  30.7 3.3 %all-gather.2.cloned.1.call-done = bf16[128,32,128]{2,1,0:T(8,128)(2,1)} async-done(((bf16[16,32,128]{2,1,0:T(8,128)(2,1)}), bf16[128,32,128]{2,1,0:T(8,128)(2,1)}) %all-gather.2.cloned.1.call-update) | async-done | bytes 1048592 | tf_op jit(solution)/shard_map/all_gather | solution.py:40
  34.0 26.1 %while.10 = (s32[]{:T(128)}, f32[4,32,16]{2,1,0:T(8,128)S(1)}, s32[16,512]{1,0:T(8,128)S(1)}, bf16[4,32,32,128]{3,2,1,0:T(8,128)(2,1)}, bf16[16,512,128]{2,1,0:T(8,128)(2,1)}, /*index=5*/s32[]{:T(128)}, f32[]{:T(128)}) while((s32[]{:T(128)}, f32[4,32,16]{2,1,0:T(8,128)S(1)}, s32[16,512]{1,0:T(8,128)S(1)}, bf16[4,32,32,128]{3,2,1,0:T(8,128)(2,1)}, ...), condition=%wide.region_5.6_spmd, body=%wide.region_2.5_spmd.sunk | while | flops 2164268544 | bytes 2574933 | solution.py:43
  34.0 6.3 %select_reduce_fusion.2 = f32[32,32,16]{1,2,0:T(8,128)S(1)} fusion(pred[16,512]{1,0:T(8,128)(4,1)S(1)} %broadcast_compare_fusion.3, bf16[16,512,128]{2,1,0:T(8,128)(2,1)} %get-tuple-element.117, bf16[4,32,32,128]{3,2,1,0:T(8,128)(2,1)} %get-tuple-element.116, s32[]{:T(128)} %get-tuple-element.106), kind=kOutput, calls=%fused_computation.1.clone.1 | convolution fusion | flops 2164244480 | bytes 2433536 | tf_op jit(solution)/shard_map/while/body/eval_jaxpr/itk,jsk->itjs/dot_general | solution.py:24
  40.3 0.1 reduce_sum.65
  40.5 6.3 %select_reduce_fusion.2 = f32[32,32,16]{1,2,0:T(8,128)S(1)} fusion(pred[16,512]{1,0:T(8,128)(4,1)S(1)} %broadcast_compare_fusion.3, bf16[16,512,128]{2,1,0:T(8,128)(2,1)} %get-tuple-element.117, bf16[4,32,32,128]{3,2,1,0:T(8,128)(2,1)} %get-tuple-element.116, s32[]{:T(128)} %get-tuple-element.106), kind=kOutput, calls=%fused_computation.1.clone.1 | convolution fusion | flops 2164244480 | bytes 2433536 | tf_op jit(solution)/shard_map/while/body/eval_jaxpr/itk,jsk->itjs/dot_general | solution.py:24
  46.8 0.1 reduce_sum.65
  47.0 6.3 %select_reduce_fusion.2 = f32[32,32,16]{1,2,0:T(8,128)S(1)} fusion(pred[16,512]{1,0:T(8,128)(4,1)S(1)} %broadcast_compare_fusion.3, bf16[16,512,128]{2,1,0:T(8,128)(2,1)} %get-tuple-element.117, bf16[4,32,32,128]{3,2,1,0:T(8,128)(2,1)} %get-tuple-element.116, s32[]{:T(128)} %get-tuple-element.106), kind=kOutput, calls=%fused_computation.1.clone.1 | convolution fusion | flops 2164244480 | bytes 2433536 | tf_op jit(solution)/shard_map/while/body/eval_jaxpr/itk,jsk->itjs/dot_general | solution.py:24
  53.5 6.3 %select_reduce_fusion.2 = f32[32,32,16]{1,2,0:T(8,128)S(1)} fusion(pred[16,512]{1,0:T(8,128)(4,1)S(1)} %broadcast_compare_fusion.3, bf16[16,512,128]{2,1,0:T(8,128)(2,1)} %get-tuple-element.117, bf16[4,32,32,128]{3,2,1,0:T(8,128)(2,1)} %get-tuple-element.116, s32[]{:T(128)} %get-tuple-element.106), kind=kOutput, calls=%fused_computation.1.clone.1 | convolution fusion | flops 2164244480 | bytes 2433536 | tf_op jit(solution)/shard_map/while/body/eval_jaxpr/itk,jsk->itjs/dot_general | solution.py:24
  59.9 0.1 reduce_sum.65
  60.1 0.7 reshape.64
  60.8 3.5 %all-to-all-start = ((f32[8,1,256]{2,1,0:T(1,128)}), f32[8,1,256]{2,1,0:T(1,128)S(1)}, u32[]{:S(2)}, u32[]{:S(2)}) async-start(f32[8,1,256]{2,1,0:T(1,128)} %reshape.64), calls=%async_computation | async-start | bytes 16384 | tf_op jit(solution)/shard_map/all_to_all | solution.py:45
  64.4 0.7 gather_fusion
  65.1 3.7 %all-to-all-done = f32[8,1,256]{2,1,0:T(1,128)S(1)} async-done(((f32[8,1,256]{2,1,0:T(1,128)}), f32[8,1,256]{2,1,0:T(1,128)S(1)}, u32[]{:S(2)}, u32[]{:S(2)}) %all-to-all-start) | async-done | bytes 8224 | tf_op jit(solution)/shard_map/all_to_all | solution.py:45
  68.8 0.5 broadcast.68
  69.3 0.7 reduce.6
  70.2 1.1 %add_reduce_fusion = (f32[]{:T(128)}, f32[16]{0:T(128)}, f32[16]{0:T(128)}) fusion(f32[16]{0:T(128)S(1)} %fusion.10, f32[16]{0:T(128)S(1)} %exponential_reduce_fusion, f32[16]{0:T(128)S(1)} %fusion.9, f32[16]{0:T(128)S(1)} %exponential_reduce_fusion.1, f32[16]{0:T(128)S(1)} %gather_fusion, f32[]{:T(128)S(6)} %copy.41), kind=kLoop, calls=%fused_computation.27 | loop fusion | flops 207 | bytes 456 | tf_op jit(solution)/shard_map/reduce_sum | solution.py:51
  71.3 13.1 %psum.7 = f32[]{:T(128)} all-reduce(f32[]{:T(128)} %get-tuple-element.61), channel_id=1, replica_groups=mesh['replica'=2,'data'=8] {'data'}, use_global_device_ids=true, to_apply=%region_11.12 | all-reduce | flops 1 | bytes 8 | tf_op jit(solution)/shard_map/psum | solution.py:51
  (27 shorter events, 0.7 us)
Async XLA Ops:
  7.2 1.2 %copy-start = (bf16[16,32,1024]{2,1,0:T(8,128)(2,1)S(1)}, bf16[16,32,1024]{2,1,0:T(8,128)(2,1)}, u32[]{:S(2)}) copy-start(bf16[16,32,1024]{2,1,0:T(8,128)(2,1)} %param.8) | copy-start | bytes 3145732
  7.2 26.8 %all-gather.2.cloned.1.call-start = ((), (), s32[]{:S(2)}) async-start(), calls=%async_computation.1 | async-start | bytes 1179648 | tf_op jit(solution)/shard_map/all_gather | solution.py:40
  24.8 9.2 %copy-start.1 = (s32[16,512]{1,0:T(8,128)S(1)}, s32[16,512]{1,0:T(8,128)}, u32[]{:S(2)}) copy-start(s32[16,512]{1,0:T(8,128)} %param.12) | copy-start | bytes 98308
  60.8 8.0 %all-to-all-start = ((f32[8,1,256]{2,1,0:T(1,128)}), f32[8,1,256]{2,1,0:T(1,128)S(1)}, u32[]{:S(2)}, u32[]{:S(2)}) async-start(f32[8,1,256]{2,1,0:T(1,128)} %reshape.64), calls=%async_computation | async-start | bytes 16384 | tf_op jit(solution)/shard_map/all_to_all | solution.py:45
Sparse Core Ops, SparseCore 0:
  11.6 22.2 all-gather.1
where the time goes:
time: 94 us; the launch traced here: 93.1 us
  matrix products  40 us (43%)
  between operations  16.6 us (18%)
  blocking collectives  13.1 us (14%)
  waiting for transfers between devices  7.04 us (7%)
  other arithmetic  6.93 us (7%)
  local copies, waits for them, and re-layouts  5.64 us (6%)
  starting transfers between devices  3.6 us (4%)
    dot_general x4, matrix products, maxsim(): jnp.einsum('itk,jsk->itjs', q_vecs, p_vecs, preferred_element_type=jnp.fl...  25.3 us
    dot_general x2, matrix products, project(): jnp.einsum('bth,hk->btk', hidden, w_proj, preferred_element_type=jnp.floa...  14.7 us
    psum x1, blocking collectives, local_loss(): group_sum = lax.psum(jnp.sum(loss_query + loss_doc), 'data')  13.1 us
    all_to_all x1, waiting for transfers between devices, local_loss(): row_scores = lax.all_to_all(col_scores, 'data', 0, 1, tiled=True)  3.72 us
    all_to_all x1, starting transfers between devices, local_loss(): row_scores = lax.all_to_all(col_scores, 'data', 0, 1, tiled=True)  3.54 us
    all_gather x1, waiting for transfers between devices, local_loss(): q_group = lax.all_gather(q_vecs, 'data', tiled=True)  3.26 us
    convert_element_type x1, other arithmetic, project(): (raw_proj / jnp.sqrt(jnp.sum(raw_proj * raw_proj, axis=-1, keepdims=True)...  2.8 us
    while x1, local copies, waits for them, and re-layouts, local_loss(): lax.map(functools.partial(maxsim, p_vecs=p_vecs, d_mask=d_mask), q_steps)  2.39 us
  transfers between devices with their start and end apart: 2, of which 2 were waited for; matrix products, arithmetic and copies ran while one was open for 21% of the time, Pallas kernels for 0%

commit v1 on v0

v1 whole, which is shorter than its diff:
```python
import functools
import jax
import jax.numpy as jnp
from jax import lax
from jax.experimental import pallas as pl
from jax.experimental.pallas import tpu as pltpu
from jax.sharding import PartitionSpec as P

MESH = pl.DeviceIdType.MESH
NT = (((1,), (1,)), ((), ()))


def unit_rows(x):
    return x * lax.rsqrt(jnp.sum(x * x, axis=1, keepdims=True))


def kernel(dims, q_hbm, d_hbm, w_hbm, qm_hbm, dm_hbm, temp_ref, lq_ref, ld_ref, lm_ref,
           w, qh, dh, qm, dm, qall, u, dmt, s_all,
           in_sem, d_sem, q_send, q_recv, s_send, s_recv):
    n, pairs, q_len, d_len, gran = dims
    q_rows = pairs * q_len
    me = lax.axis_index('data')
    core = lax.rem(me, 2)
    chip = me // 2
    chips = n // 2
    partner = chip * 2 + (1 - core)

    def dev(dc, other):
        c = lax.rem(chip + dc, chips)
        return c * 2 + ((1 - core) if other else core)

    barrier = pltpu.get_barrier_semaphore()
    for o in range(1, n):
        pl.semaphore_signal(barrier, inc=1, device_id={'data': lax.rem(me + o, n)}, device_id_type=MESH)

    ins = [pltpu.make_async_copy(src, dst, in_sem.at[i]) for i, (src, dst) in enumerate(
        ((w_hbm, w), (q_hbm, qh), (qm_hbm, qm), (dm_hbm, dm)))]
    for c in ins:
        c.start()
    grows = gran * d_len
    n_gran = pairs // gran
    d_copies = []
    for g in range(n_gran):
        c = pltpu.make_async_copy(d_hbm.at[pl.ds(g * grows, grows)], dh.at[pl.ds(g * grows, grows)], d_sem.at[g])
        c.start()
        d_copies.append(c)

    for c in ins:
        c.wait()

    row = lax.broadcasted_iota(jnp.int32, (q_rows, pairs), 0)
    own = (row // q_len == lax.broadcasted_iota(jnp.int32, (q_rows, pairs), 1)).astype(jnp.bfloat16)
    spread = jnp.dot(own, qm[...].astype(jnp.bfloat16), preferred_element_type=jnp.float32)
    row = lax.broadcasted_iota(jnp.int32, (q_rows, q_len), 0)
    tok = lax.broadcasted_iota(jnp.int32, (q_rows, q_len), 1)
    q_keep = jnp.sum(jnp.where(row % q_len == tok, spread, 0.0), axis=1, keepdims=True)
    xq = unit_rows(jnp.dot(qh[...], w[...], preferred_element_type=jnp.float32))
    qall[me] = jnp.where(q_keep > 0.5, xq, 0.0).astype(jnp.bfloat16)

    dmf = dm[...].astype(jnp.float32)
    dmt[...] = dmf.T
    pos = lax.broadcasted_iota(jnp.int32, (pairs, d_len), 1).astype(jnp.float32)
    first = jnp.min(jnp.where(dmf > 0.5, pos, float(d_len)), axis=1, keepdims=True)

    pl.semaphore_wait(barrier, n - 1)

    def send(slot, target, i):
        c = pltpu.make_async_remote_copy(
            src_ref=qall.at[slot], dst_ref=qall.at[slot], send_sem=q_send.at[i], recv_sem=q_recv.at[slot],
            device_id={'data': target}, device_id_type=MESH)
        c.start()
        return c

    def arrive(slot):
        pltpu.make_async_remote_copy(
            src_ref=qall.at[slot], dst_ref=qall.at[slot], send_sem=q_send.at[0], recv_sem=q_recv.at[slot],
            device_id={'data': partner}, device_id_type=MESH).wait_recv()

    hops = [1, chips - 1] + list(range(2, chips - 1))
    sends = [send(me, dev(h, False), i) for i, h in enumerate(hops)]
    sends.append(send(me, partner, len(hops)))

    def project(g):
        x = unit_rows(jnp.dot(dh[pl.ds(g * grows, grows), :], w[...], preferred_element_type=jnp.float32))
        for k in range(gran):
            j = g * gran + k
            xj = x[k * d_len:(k + 1) * d_len]
            at = lax.broadcasted_iota(jnp.int32, (d_len, 1), 0).astype(jnp.float32)
            rep = jnp.sum(jnp.where(at == first[j:j + 1, :], xj, 0.0), axis=0, keepdims=True)
            keep = dmt[:, j:j + 1] > 0.5
            u[pl.ds(j * d_len, d_len), :] = jnp.where(keep, xj, rep).astype(jnp.bfloat16)

    def best_of(slot, j):
        sim = lax.dot_general(u[pl.ds(j * d_len, d_len), :], qall[slot], NT, preferred_element_type=jnp.float32)
        return jnp.max(sim, axis=0, keepdims=True)

    sel = (lax.broadcasted_iota(jnp.int32, (q_rows, 128), 0) // q_len
           == lax.broadcasted_iota(jnp.int32, (q_rows, 128), 1)).astype(jnp.bfloat16)

    def scores(slot, rows):
        best = jnp.concatenate(rows, axis=0)
        hi = best.astype(jnp.bfloat16)
        r1 = best - hi.astype(jnp.float32)
        mid = r1.astype(jnp.bfloat16)
        lo = (r1 - mid.astype(jnp.float32)).astype(jnp.bfloat16)
        s = jnp.dot(hi, sel, preferred_element_type=jnp.float32)
        s = s + (jnp.dot(mid, sel, preferred_element_type=jnp.float32)
                 + jnp.dot(lo, sel, preferred_element_type=jnp.float32))
        return pltpu.roll(s, slot * pairs, 1)

    rows = []
    for g in range(n_gran):
        d_copies[g].wait()
        project(g)
        if g > 0:
            rows += [best_of(me, (g - 1) * gran + k) for k in range(gran)]
    rows += [best_of(me, (n_gran - 1) * gran + k) for k in range(gran)]
    total = scores(me, rows)

    def forward(h, i):
        slot = dev(h, False)
        arrive(slot)
        sends.append(send(slot, partner, i))

    forward(hops[0], n - chips + 0)
    forward(hops[1], n - chips + 1)
    arrive(partner)
    total += scores(partner, [best_of(partner, j) for j in range(pairs)])
    slot = dev(hops[0], False)
    total += scores(slot, [best_of(slot, j) for j in range(pairs)])
    slot = dev(hops[1], False)
    total += scores(slot, [best_of(slot, j) for j in range(pairs)])
    for i, h in enumerate(hops[2:]):
        forward(h, n - chips + 2 + i)
    for h in hops[:2]:
        slot = dev(h, True)
        arrive(slot)
        total += scores(slot, [best_of(slot, j) for j in range(pairs)])
    for h in hops[2:]:
        slot = dev(h, False)
        total += scores(slot, [best_of(slot, j) for j in range(pairs)])
    for h in hops[2:]:
        slot = dev(h, True)
        arrive(slot)
        total += scores(slot, [best_of(slot, j) for j in range(pairs)])

    mine = pl.ds(pl.multiple_of(me * pairs, pairs), pairs)
    s_all[mine, :] = total
    s_sends = []
    for o in range(1, n):
        c = pltpu.make_async_remote_copy(
            src_ref=s_all.at[mine], dst_ref=s_all.at[mine], send_sem=s_send.at[o], recv_sem=s_recv.at[me],
            device_id={'data': lax.rem(me + o, n)}, device_id_type=MESH)
        c.start()
        s_sends.append(c)
    for c in sends:
        c.wait_send()
    for o in range(1, n):
        src = lax.rem(me + o, n)
        theirs = pl.ds(pl.multiple_of(src * pairs, pairs), pairs)
        pltpu.make_async_remote_copy(
            src_ref=s_all.at[theirs], dst_ref=s_all.at[theirs], send_sem=s_send.at[o], recv_sem=s_recv.at[src],
            device_id={'data': src}, device_id_type=MESH).wait_recv()
    for c in s_sends:
        c.wait_send()

    z = s_all[...] / temp_ref[0]
    size = n * pairs
    diag = (lax.broadcasted_iota(jnp.int32, (size, size), 0) == lax.broadcasted_iota(jnp.int32, (size, size), 1))
    pos_logit = jnp.sum(jnp.where(diag, z, 0.0), axis=0, keepdims=True)

    def lse(v):
        top = jnp.max(v, axis=0, keepdims=True)
        return jnp.log(jnp.sum(jnp.exp(v - top), axis=0, keepdims=True)) + top

    loss_q = lse(z) - pos_logit
    loss_d = lse(z.T) - pos_logit
    lm_ref[0] = jnp.sum(loss_q + loss_d) / (2 * size)
    back = lax.rem(size - me * pairs, size)
    lq_ref[...] = pltpu.roll(loss_q, back, 1)[:, :pairs]
    ld_ref[...] = pltpu.roll(loss_d, back, 1)[:, :pairs]


def solution(mesh):
    n = mesh.shape['data']
    batch_spec = P(('replica', 'data'))

    def local_loss(q_hidden, d_hidden, w_proj, q_mask, d_mask, temperature):
        pairs, q_len, hidden = q_hidden.shape
        d_len = d_hidden.shape[1]
        k = w_proj.shape[1]
        gran = 2
        any_ = pl.BlockSpec(memory_space=pl.ANY)
        lq, ld, lm = pl.pallas_call(
            functools.partial(kernel, (n, pairs, q_len, d_len, gran)),
            out_shape=(jax.ShapeDtypeStruct((1, pairs), jnp.float32), jax.ShapeDtypeStruct((1, pairs), jnp.float32),
                       jax.ShapeDtypeStruct((1,), jnp.float32)),
            in_specs=[any_] * 5 + [pl.BlockSpec(memory_space=pltpu.SMEM)],
            out_specs=(pl.BlockSpec(memory_space=pltpu.VMEM), pl.BlockSpec(memory_space=pltpu.VMEM),
                       pl.BlockSpec(memory_space=pltpu.SMEM)),
            scratch_shapes=[
                pltpu.VMEM((hidden, k), jnp.bfloat16),
                pltpu.VMEM((pairs * q_len, hidden), jnp.bfloat16),
                pltpu.VMEM((pairs * d_len, hidden), jnp.bfloat16),
                pltpu.VMEM((pairs, q_len), jnp.int32),
                pltpu.VMEM((pairs, d_len), jnp.int32),
                pltpu.VMEM((n, pairs * q_len, k), jnp.bfloat16),
                pltpu.VMEM((pairs * d_len, k), jnp.bfloat16),
                pltpu.VMEM((d_len, pairs), jnp.float32),
                pltpu.VMEM((n * pairs, n * pairs), jnp.float32),
                pltpu.SemaphoreType.DMA((4,)),
                pltpu.SemaphoreType.DMA((pairs // gran,)),
                pltpu.SemaphoreType.DMA((n,)),
                pltpu.SemaphoreType.DMA((n,)),
                pltpu.SemaphoreType.DMA((n,)),
                pltpu.SemaphoreType.DMA((n,)),
            ],
            compiler_params=pltpu.CompilerParams(
                collective_id=0, has_side_effects=True),
        )(q_hidden.reshape(pairs * q_len, hidden), d_hidden.reshape(pairs * d_len, hidden), w_proj,
          q_mask, d_mask, temperature.reshape(1))
        return lq.reshape(pairs), ld.reshape(pairs), lm

    return jax.shard_map(local_loss, mesh=mesh, in_specs=(batch_spec, batch_spec, P(), batch_spec, batch_spec, P()),
                         out_specs=(batch_spec, batch_spec, P('replica')), check_vma=False)
```

time: 94 us -> 48.5 us (0.52)
  Pallas kernels: 0 us -> 43.1 us
  matrix products: 40 us -> 0 us
  between operations: 16.6 us -> 3.05 us
  blocking collectives: 13.1 us -> 0 us
  waiting for transfers between devices: 7.04 us -> 0 us
  other arithmetic: 6.93 us -> 0 us
  starting transfers between devices: 3.6 us -> 0 us
  local copies, waits for them, and re-layouts: 5.64 us -> 2.25 us
    pallas_call x0 -> x1, Pallas kernels: none -> 43.1 us  [local_loss(): pl.pallas_call(functools.partial(kernel, (n, pairs, q_len, d_len, gran)),...]
    dot_general x6 -> x0, matrix products: 40 us -> none  [the longest x4 25.3 us: maxsim(): jnp.einsum('itk,jsk->itjs', q_vecs, p_vecs, preferred_element_type=jnp.fl...]
    psum x1 -> x0, blocking collectives: 13.1 us -> none  [local_loss(): group_sum = lax.psum(jnp.sum(loss_query + loss_doc), 'data')]
    all_to_all x1 -> x0, waiting for transfers between devices: 3.72 us -> none  [local_loss(): row_scores = lax.all_to_all(col_scores, 'data', 0, 1, tiled=True)]
    all_to_all x1 -> x0, starting transfers between devices: 3.54 us -> none  [local_loss(): row_scores = lax.all_to_all(col_scores, 'data', 0, 1, tiled=True)]
    all_gather x1 -> x0, waiting for transfers between devices: 3.26 us -> none  [local_loss(): q_group = lax.all_gather(q_vecs, 'data', tiled=True)]
    convert_element_type x1 -> x0, other arithmetic: 2.8 us -> none  [project(): (raw_proj / jnp.sqrt(jnp.sum(raw_proj * raw_proj, axis=-1, keepdims=True)...]
    while x1 -> x0, local copies, waits for them, and re-layouts: 2.39 us -> none  [local_loss(): lax.map(functools.partial(maxsim, p_vecs=p_vecs, d_mask=d_mask), q_steps)]
  transfers between devices with their start and end apart: 2 -> 0, of which waited for: 2 -> 0; matrix products, arithmetic and copies ran while one was open for 21% -> 0% of each run, Pallas kernels for 0% -> 0%
where the time goes in v1:
time: 48.5 us; the launch traced here: 48.4 us
  Pallas kernels  43.1 us (89%)
  between operations  3.05 us (6%)
  local copies, waits for them, and re-layouts  2.25 us (5%)
    pallas_call x1, Pallas kernels, local_loss(): pl.pallas_call(functools.partial(kernel, (n, pairs, q_len, d_len, gran)),...  43.1 us
    unnamed x2, local copies, waits for them, and re-layouts  2.25 us

profile of v1, /device:TPU:113, one launch (start us, length us, event | category | flops | bytes accessed | tf_op | source)
XLA Modules:
  0.0 48.4 jit_solution(4809969052349903724)
XLA Ops:
  1.3 43.1 %shard_map.85 = (f32[1,16]{1,0:T(1,128)}, f32[1,16]{1,0:T(1,128)}, f32[1]{0:T(128)}) custom-call(bf16[512,1024]{1,0:T(8,128)(2,1)} %bitcast.7, bf16[8192,1024]{1,0:T(8,128)(2,1)} %bitcast.6, bf16[1024,128]{1,0:T(8,128)(2,1)} %w_hbm.1, s32[16,32]{1,0:T(8,128)} %qm_hbm.1, s32[16,512]{1,0:T(8,128)} %dm_hbm.1, f32[1]{0:T(128)} %bitcast.5.temp_ref), custom_call_target="tpu_custom_call" | custom-call | tf_op jit(solution)/shard_map/pallas_call | solution.py:194
  44.4 1.1 %copy.13 = f32[16]{0:T(128)} copy(f32[16]{0:T(128)} %bitcast.9) | data formatting | bytes 128
  45.5 1.1 %copy.14 = f32[16]{0:T(128)} copy(f32[16]{0:T(128)} %bitcast.8) | data formatting | bytes 128

commit v2 on v1

--- a/solution.py
+++ b/solution.py
@@ -7,15 +7,14 @@
 from jax.sharding import PartitionSpec as P
 
 MESH = pl.DeviceIdType.MESH
-NT = (((1,), (1,)), ((), ()))
 
 
 def unit_rows(x):
     return x * lax.rsqrt(jnp.sum(x * x, axis=1, keepdims=True))
 
 
-def kernel(dims, q_hbm, d_hbm, w_hbm, qm_hbm, dm_hbm, temp_ref, lq_ref, ld_ref, lm_ref,
-           w, qh, dh, qm, dm, qall, u, dmt, s_all,
+def kernel(dims, q_hbm, d_hbm, w_hbm, qm_hbm, dm_hbm, s_all,
+           w, qh, dh, qm, dm, qall, u, dmt,
            in_sem, d_sem, q_send, q_recv, s_send, s_recv):
     n, pairs, q_len, d_len, gran = dims
     q_rows = pairs * q_len
@@ -42,8 +41,9 @@
     d_copies = []
     for g in range(n_gran):
         c = pltpu.make_async_copy(d_hbm.at[pl.ds(g * grows, grows)], dh.at[pl.ds(g * grows, grows)], d_sem.at[g])
-        c.start()
         d_copies.append(c)
+    for c in d_copies[:2]:
+        c.start()
 
     for c in ins:
         c.wait()
@@ -55,15 +55,13 @@
     tok = lax.broadcasted_iota(jnp.int32, (q_rows, q_len), 1)
     q_keep = jnp.sum(jnp.where(row % q_len == tok, spread, 0.0), axis=1, keepdims=True)
     xq = unit_rows(jnp.dot(qh[...], w[...], preferred_element_type=jnp.float32))
-    qall[me] = jnp.where(q_keep > 0.5, xq, 0.0).astype(jnp.bfloat16)
+    qall[me] = jnp.where(q_keep > 0.5, xq, 0.0).T.astype(jnp.bfloat16)
 
     dmf = dm[...].astype(jnp.float32)
     dmt[...] = dmf.T
     pos = lax.broadcasted_iota(jnp.int32, (pairs, d_len), 1).astype(jnp.float32)
     first = jnp.min(jnp.where(dmf > 0.5, pos, float(d_len)), axis=1, keepdims=True)
 
-    pl.semaphore_wait(barrier, n - 1)
-
     def send(slot, target, i):
         c = pltpu.make_async_remote_copy(
             src_ref=qall.at[slot], dst_ref=qall.at[slot], send_sem=q_send.at[i], recv_sem=q_recv.at[slot],
@@ -77,8 +75,7 @@
             device_id={'data': partner}, device_id_type=MESH).wait_recv()
 
     hops = [1, chips - 1] + list(range(2, chips - 1))
-    sends = [send(me, dev(h, False), i) for i, h in enumerate(hops)]
-    sends.append(send(me, partner, len(hops)))
+    sends = []
 
     def project(g):
         x = unit_rows(jnp.dot(dh[pl.ds(g * grows, grows), :], w[...], preferred_element_type=jnp.float32))
@@ -91,7 +88,7 @@
             u[pl.ds(j * d_len, d_len), :] = jnp.where(keep, xj, rep).astype(jnp.bfloat16)
 
     def best_of(slot, j):
-        sim = lax.dot_general(u[pl.ds(j * d_len, d_len), :], qall[slot], NT, preferred_element_type=jnp.float32)
+        sim = jnp.dot(u[pl.ds(j * d_len, d_len), :], qall[slot], preferred_element_type=jnp.float32)
         return jnp.max(sim, axis=0, keepdims=True)
 
     sel = (lax.broadcasted_iota(jnp.int32, (q_rows, 128), 0) // q_len
@@ -111,8 +108,14 @@
     rows = []
     for g in range(n_gran):
         d_copies[g].wait()
+        if g + 2 < n_gran:
+            d_copies[g + 2].start()
         project(g)
-        if g > 0:
+        if g == 0:
+            pl.semaphore_wait(barrier, n - 1)
+            sends += [send(me, dev(h, False), i) for i, h in enumerate(hops)]
+            sends.append(send(me, partner, len(hops)))
+        else:
             rows += [best_of(me, (g - 1) * gran + k) for k in range(gran)]
     rows += [best_of(me, (n_gran - 1) * gran + k) for k in range(gran)]
     total = scores(me, rows)
@@ -122,27 +125,19 @@
         arrive(slot)
         sends.append(send(slot, partner, i))
 
-    forward(hops[0], n - chips + 0)
-    forward(hops[1], n - chips + 1)
+    def blocks(slots):
+        return functools.reduce(lambda x, y: x + y, [
+            scores(slot, [best_of(slot, j) for j in range(pairs)]) for slot in slots])
+
+    forward(hops[0], len(hops) + 1)
+    forward(hops[1], len(hops) + 2)
     arrive(partner)
-    total += scores(partner, [best_of(partner, j) for j in range(pairs)])
-    slot = dev(hops[0], False)
-    total += scores(slot, [best_of(slot, j) for j in range(pairs)])
-    slot = dev(hops[1], False)
-    total += scores(slot, [best_of(slot, j) for j in range(pairs)])
+    total += blocks([partner] + [dev(h, False) for h in hops[:2]])
     for i, h in enumerate(hops[2:]):
-        forward(h, n - chips + 2 + i)
-    for h in hops[:2]:
-        slot = dev(h, True)
-        arrive(slot)
-        total += scores(slot, [best_of(slot, j) for j in range(pairs)])
-    for h in hops[2:]:
-        slot = dev(h, False)
-        total += scores(slot, [best_of(slot, j) for j in range(pairs)])
-    for h in hops[2:]:
-        slot = dev(h, True)
-        arrive(slot)
-        total += scores(slot, [best_of(slot, j) for j in range(pairs)])
+        forward(h, len(hops) + 3 + i)
+    for h in hops:
+        arrive(dev(h, True))
+    total += blocks([dev(h, True) for h in hops[:2]] + [dev(h, o) for h in hops[2:] for o in (False, True)])
 
     mine = pl.ds(pl.multiple_of(me * pairs, pairs), pairs)
     s_all[mine, :] = total
@@ -164,8 +159,11 @@
     for c in s_sends:
         c.wait_send()
 
-    z = s_all[...] / temp_ref[0]
-    size = n * pairs
+
+def losses(pairs, s_ref, temp_ref, lq_ref, ld_ref, lm_ref):
+    z = s_ref[...] / temp_ref[0]
+    size = s_ref.shape[0]
+    me = lax.axis_index('data')
     diag = (lax.broadcasted_iota(jnp.int32, (size, size), 0) == lax.broadcasted_iota(jnp.int32, (size, size), 1))
     pos_logit = jnp.sum(jnp.where(diag, z, 0.0), axis=0, keepdims=True)
 
@@ -189,25 +187,23 @@
         pairs, q_len, hidden = q_hidden.shape
         d_len = d_hidden.shape[1]
         k = w_proj.shape[1]
-        gran = 2
+        gran = 4
         any_ = pl.BlockSpec(memory_space=pl.ANY)
-        lq, ld, lm = pl.pallas_call(
+        vmem, smem = pl.BlockSpec(memory_space=pltpu.VMEM), pl.BlockSpec(memory_space=pltpu.SMEM)
+        scores = pl.pallas_call(
             functools.partial(kernel, (n, pairs, q_len, d_len, gran)),
-            out_shape=(jax.ShapeDtypeStruct((1, pairs), jnp.float32), jax.ShapeDtypeStruct((1, pairs), jnp.float32),
-                       jax.ShapeDtypeStruct((1,), jnp.float32)),
-            in_specs=[any_] * 5 + [pl.BlockSpec(memory_space=pltpu.SMEM)],
-            out_specs=(pl.BlockSpec(memory_space=pltpu.VMEM), pl.BlockSpec(memory_space=pltpu.VMEM),
-                       pl.BlockSpec(memory_space=pltpu.SMEM)),
+            out_shape=jax.ShapeDtypeStruct((n * pairs, n * pairs), jnp.float32),
+            in_specs=[any_] * 5,
+            out_specs=vmem,
             scratch_shapes=[
                 pltpu.VMEM((hidden, k), jnp.bfloat16),
                 pltpu.VMEM((pairs * q_len, hidden), jnp.bfloat16),
                 pltpu.VMEM((pairs * d_len, hidden), jnp.bfloat16),
                 pltpu.VMEM((pairs, q_len), jnp.int32),
                 pltpu.VMEM((pairs, d_len), jnp.int32),
-                pltpu.VMEM((n, pairs * q_len, k), jnp.bfloat16),
+                pltpu.VMEM((n, k, pairs * q_len), jnp.bfloat16),
                 pltpu.VMEM((pairs * d_len, k), jnp.bfloat16),
                 pltpu.VMEM((d_len, pairs), jnp.float32),
-                pltpu.VMEM((n * pairs, n * pairs), jnp.float32),
                 pltpu.SemaphoreType.DMA((4,)),
                 pltpu.SemaphoreType.DMA((pairs // gran,)),
                 pltpu.SemaphoreType.DMA((n,)),
@@ -218,7 +214,14 @@
             compiler_params=pltpu.CompilerParams(
                 collective_id=0, has_side_effects=True),
         )(q_hidden.reshape(pairs * q_len, hidden), d_hidden.reshape(pairs * d_len, hidden), w_proj,
-          q_mask, d_mask, temperature.reshape(1))
+          q_mask, d_mask)
+        lq, ld, lm = pl.pallas_call(
+            functools.partial(losses, pairs),
+            out_shape=(jax.ShapeDtypeStruct((1, pairs), jnp.float32), jax.ShapeDtypeStruct((1, pairs), jnp.float32),
+                       jax.ShapeDtypeStruct((1,), jnp.float32)),
+            in_specs=[vmem, smem],
+            out_specs=(vmem, vmem, smem),
+        )(scores, temperature.reshape(1))
         return lq.reshape(pairs), ld.reshape(pairs), lm
 
     return jax.shard_map(local_loss, mesh=mesh, in_specs=(batch_spec, batch_spec, P(), batch_spec, batch_spec, P()),

time: 48.5 us -> 43 us (0.89)
  local copies, waits for them, and re-layouts: 2.25 us -> 0 us
  Pallas kernels: 43.1 us -> 41.4 us
  between operations: 3.05 us -> 1.45 us
    pallas_call x1, Pallas kernels: 43.1 us -> 39.8 us  [local_loss(): pl.pallas_call(functools.partial(kernel, (n, pairs, q_len, d_len, gran)),...]
    unnamed x2 -> x0, local copies, waits for them, and re-layouts: 2.25 us -> none
    pallas_call x0 -> x1, Pallas kernels: none -> 1.63 us  [local_loss(): pl.pallas_call(functools.partial(losses, pairs), out_shape=(jax.ShapeDtyp...]
where the time goes in v2:
time: 43 us; the launch traced here: 42.9 us
  Pallas kernels  41.4 us (96%)
  between operations  1.45 us (3%)
    pallas_call x1, Pallas kernels, local_loss(): pl.pallas_call(functools.partial(kernel, (n, pairs, q_len, d_len, gran)),...  39.8 us
    pallas_call x1, Pallas kernels, local_loss(): pl.pallas_call(functools.partial(losses, pairs), out_shape=(jax.ShapeDtyp...  1.63 us

profile of v2, /device:TPU:113, one launch (start us, length us, event | category | flops | bytes accessed | tf_op | source)
XLA Modules:
  0.0 42.9 jit_solution(8041079374713503254)
XLA Ops:
  1.3 39.8 %shard_map.85.s_ref = f32[128,128]{1,0:T(8,128)} custom-call(bf16[512,1024]{1,0:T(8,128)(2,1)} %bitcast.7, bf16[8192,1024]{1,0:T(8,128)(2,1)} %bitcast.6, bf16[1024,128]{1,0:T(8,128)(2,1)} %w_hbm.1, s32[16,32]{1,0:T(8,128)} %qm_hbm.1, s32[16,512]{1,0:T(8,128)} %dm_hbm.1), custom_call_target="tpu_custom_call" | custom-call | tf_op jit(solution)/shard_map/pallas_call | solution.py:193
  41.1 1.6 %shard_map.86 = (f32[1,16]{1,0:T(1,128)}, f32[1,16]{1,0:T(1,128)}, f32[1]{0:T(128)}) custom-call(f32[128,128]{1,0:T(8,128)} %shard_map.85.s_ref, f32[1]{0:T(128)} %bitcast.5.temp_ref), custom_call_target="tpu_custom_call" | custom-call | tf_op jit(solution)/shard_map/pallas_call | solution.py:218

commit v3 on v2

--- a/solution.py
+++ b/solution.py
@@ -14,7 +14,7 @@
 
 
 def kernel(dims, q_hbm, d_hbm, w_hbm, qm_hbm, dm_hbm, s_all,
-           w, qh, dh, qm, dm, qall, u, dmt,
+           w, qh, dh, qm, dm, qall, u, bias,
            in_sem, d_sem, q_send, q_recv, s_send, s_recv):
     n, pairs, q_len, d_len, gran = dims
     q_rows = pairs * q_len
@@ -28,12 +28,8 @@
         c = lax.rem(chip + dc, chips)
         return c * 2 + ((1 - core) if other else core)
 
-    barrier = pltpu.get_barrier_semaphore()
-    for o in range(1, n):
-        pl.semaphore_signal(barrier, inc=1, device_id={'data': lax.rem(me + o, n)}, device_id_type=MESH)
-
     ins = [pltpu.make_async_copy(src, dst, in_sem.at[i]) for i, (src, dst) in enumerate(
-        ((w_hbm, w), (q_hbm, qh), (qm_hbm, qm), (dm_hbm, dm)))]
+        ((dm_hbm, dm), (qm_hbm, qm), (w_hbm, w), (q_hbm, qh)))]
     for c in ins:
         c.start()
     grows = gran * d_len
@@ -45,22 +41,19 @@
     for c in d_copies[:2]:
         c.start()
 
-    for c in ins:
+    barrier = pltpu.get_barrier_semaphore()
+    for o in range(1, n):
+        pl.semaphore_signal(barrier, inc=1, device_id={'data': lax.rem(me + o, n)}, device_id_type=MESH)
+
+    for c in ins[:2]:
         c.wait()
 
-    row = lax.broadcasted_iota(jnp.int32, (q_rows, pairs), 0)
-    own = (row // q_len == lax.broadcasted_iota(jnp.int32, (q_rows, pairs), 1)).astype(jnp.bfloat16)
-    spread = jnp.dot(own, qm[...].astype(jnp.bfloat16), preferred_element_type=jnp.float32)
-    row = lax.broadcasted_iota(jnp.int32, (q_rows, q_len), 0)
-    tok = lax.broadcasted_iota(jnp.int32, (q_rows, q_len), 1)
-    q_keep = jnp.sum(jnp.where(row % q_len == tok, spread, 0.0), axis=1, keepdims=True)
-    xq = unit_rows(jnp.dot(qh[...], w[...], preferred_element_type=jnp.float32))
-    qall[me] = jnp.where(q_keep > 0.5, xq, 0.0).T.astype(jnp.bfloat16)
-
-    dmf = dm[...].astype(jnp.float32)
-    dmt[...] = dmf.T
-    pos = lax.broadcasted_iota(jnp.int32, (pairs, d_len), 1).astype(jnp.float32)
-    first = jnp.min(jnp.where(dmf > 0.5, pos, float(d_len)), axis=1, keepdims=True)
+    bias_t = jnp.where(dm[...] == 1, 0.0, -jnp.inf).T
+    for j in range(pairs):
+        bias[pl.ds(j * d_len, d_len), :] = jnp.broadcast_to(bias_t[:, j:j + 1], (d_len, 128))
+
+    for c in ins[2:]:
+        c.wait()
 
     def send(slot, target, i):
         c = pltpu.make_async_remote_copy(
@@ -77,19 +70,26 @@
     hops = [1, chips - 1] + list(range(2, chips - 1))
     sends = []
 
+    def project_queries():
+        row = lax.broadcasted_iota(jnp.int32, (q_rows, pairs), 0)
+        own = (row // q_len == lax.broadcasted_iota(jnp.int32, (q_rows, pairs), 1)).astype(jnp.bfloat16)
+        spread = jnp.dot(own, qm[...].astype(jnp.bfloat16), preferred_element_type=jnp.float32)
+        row = lax.broadcasted_iota(jnp.int32, (q_rows, q_len), 0)
+        tok = lax.broadcasted_iota(jnp.int32, (q_rows, q_len), 1)
+        q_keep = jnp.sum(jnp.where(row % q_len == tok, spread, 0.0), axis=1, keepdims=True)
+        xq = unit_rows(jnp.dot(qh[...], w[...], preferred_element_type=jnp.float32))
+        qall[me] = jnp.where(q_keep > 0.5, xq, 0.0).T.astype(jnp.bfloat16)
+
     def project(g):
-        x = unit_rows(jnp.dot(dh[pl.ds(g * grows, grows), :], w[...], preferred_element_type=jnp.float32))
-        for k in range(gran):
-            j = g * gran + k
-            xj = x[k * d_len:(k + 1) * d_len]
-            at = lax.broadcasted_iota(jnp.int32, (d_len, 1), 0).astype(jnp.float32)
-            rep = jnp.sum(jnp.where(at == first[j:j + 1, :], xj, 0.0), axis=0, keepdims=True)
-            keep = dmt[:, j:j + 1] > 0.5
-            u[pl.ds(j * d_len, d_len), :] = jnp.where(keep, xj, rep).astype(jnp.bfloat16)
+        here = pl.ds(g * grows, grows)
+        x = jnp.dot(dh[here, :], w[...], preferred_element_type=jnp.float32)
+        r = lax.rsqrt(jnp.sum(x * x, axis=1, keepdims=True))
+        u[here, :] = (x * jnp.where(bias[here, :] == 0.0, r, 0.0)).astype(jnp.bfloat16)
 
     def best_of(slot, j):
-        sim = jnp.dot(u[pl.ds(j * d_len, d_len), :], qall[slot], preferred_element_type=jnp.float32)
-        return jnp.max(sim, axis=0, keepdims=True)
+        here = pl.ds(j * d_len, d_len)
+        sim = jnp.dot(u[here, :], qall[slot], preferred_element_type=jnp.float32)
+        return jnp.max(sim + jnp.concatenate([bias[here, :]] * (q_rows // 128), axis=1), axis=0, keepdims=True)
 
     sel = (lax.broadcasted_iota(jnp.int32, (q_rows, 128), 0) // q_len
            == lax.broadcasted_iota(jnp.int32, (q_rows, 128), 1)).astype(jnp.bfloat16)
@@ -110,6 +110,8 @@
         d_copies[g].wait()
         if g + 2 < n_gran:
             d_copies[g + 2].start()
+        if g == 0:
+            project_queries()
         project(g)
         if g == 0:
             pl.semaphore_wait(barrier, n - 1)
@@ -129,15 +131,18 @@
         return functools.reduce(lambda x, y: x + y, [
             scores(slot, [best_of(slot, j) for j in range(pairs)]) for slot in slots])
 
-    forward(hops[0], len(hops) + 1)
-    forward(hops[1], len(hops) + 2)
+    for i, h in enumerate(hops[:2]):
+        forward(h, len(hops) + 1 + i)
     arrive(partner)
     total += blocks([partner] + [dev(h, False) for h in hops[:2]])
     for i, h in enumerate(hops[2:]):
         forward(h, len(hops) + 3 + i)
-    for h in hops:
+    for h in hops[:2]:
         arrive(dev(h, True))
-    total += blocks([dev(h, True) for h in hops[:2]] + [dev(h, o) for h in hops[2:] for o in (False, True)])
+    total += blocks([dev(h, True) for h in hops[:2]])
+    for h in hops[2:]:
+        arrive(dev(h, True))
+    total += blocks([dev(h, o) for h in hops[2:] for o in (False, True)])
 
     mine = pl.ds(pl.multiple_of(me * pairs, pairs), pairs)
     s_all[mine, :] = total
@@ -187,13 +192,13 @@
         pairs, q_len, hidden = q_hidden.shape
         d_len = d_hidden.shape[1]
         k = w_proj.shape[1]
-        gran = 4
-        any_ = pl.BlockSpec(memory_space=pl.ANY)
+        gran = 2
+        hbm = pl.BlockSpec(memory_space=pltpu.HBM)
         vmem, smem = pl.BlockSpec(memory_space=pltpu.VMEM), pl.BlockSpec(memory_space=pltpu.SMEM)
         scores = pl.pallas_call(
             functools.partial(kernel, (n, pairs, q_len, d_len, gran)),
             out_shape=jax.ShapeDtypeStruct((n * pairs, n * pairs), jnp.float32),
-            in_specs=[any_] * 5,
+            in_specs=[hbm] * 5,
             out_specs=vmem,
             scratch_shapes=[
                 pltpu.VMEM((hidden, k), jnp.bfloat16),
@@ -203,7 +208,7 @@
                 pltpu.VMEM((pairs, d_len), jnp.int32),
                 pltpu.VMEM((n, k, pairs * q_len), jnp.bfloat16),
                 pltpu.VMEM((pairs * d_len, k), jnp.bfloat16),
-                pltpu.VMEM((d_len, pairs), jnp.float32),
+                pltpu.VMEM((pairs * d_len, 128), jnp.float32),
                 pltpu.SemaphoreType.DMA((4,)),
                 pltpu.SemaphoreType.DMA((pairs // gran,)),
                 pltpu.SemaphoreType.DMA((n,)),

time: 43 us -> 41.1 us (0.956)
  Pallas kernels: 41.4 us -> 39.5 us
    pallas_call x1, Pallas kernels: 39.8 us -> 37.9 us  [local_loss(): pl.pallas_call(functools.partial(kernel, (n, pairs, q_len, d_len, gran)),...]
where the time goes in v3:
time: 41.1 us; the launch traced here: 41 us
  Pallas kernels  39.5 us (96%)
  between operations  1.45 us (4%)
    pallas_call x1, Pallas kernels, local_loss(): pl.pallas_call(functools.partial(kernel, (n, pairs, q_len, d_len, gran)),...  37.9 us
    pallas_call x1, Pallas kernels, local_loss(): pl.pallas_call(functools.partial(losses, pairs), out_shape=(jax.ShapeDtyp...  1.63 us

profile of v3, /device:TPU:113, one launch (start us, length us, event | category | flops | bytes accessed | tf_op | source)
XLA Modules:
  0.0 41.0 jit_solution(13306406547256978270)
XLA Ops:
  1.3 37.9 %shard_map.85.s_ref = f32[128,128]{1,0:T(8,128)} custom-call(bf16[512,1024]{1,0:T(8,128)(2,1)} %bitcast.7, bf16[8192,1024]{1,0:T(8,128)(2,1)} %bitcast.6, bf16[1024,128]{1,0:T(8,128)(2,1)} %w_hbm.1, s32[16,32]{1,0:T(8,128)} %qm_hbm.1, s32[16,512]{1,0:T(8,128)} %dm_hbm.1), custom_call_target="tpu_custom_call" | custom-call | tf_op jit(solution)/shard_map/pallas_call | solution.py:198
  39.2 1.6 %shard_map.86 = (f32[1,16]{1,0:T(1,128)}, f32[1,16]{1,0:T(1,128)}, f32[1]{0:T(128)}) custom-call(f32[128,128]{1,0:T(8,128)} %shard_map.85.s_ref, f32[1]{0:T(128)} %bitcast.5.temp_ref), custom_call_target="tpu_custom_call" | custom-call | tf_op jit(solution)/shard_map/pallas_call | solution.py:223

commit v4 on v3

--- a/solution.py
+++ b/solution.py
@@ -94,16 +94,17 @@
     sel = (lax.broadcasted_iota(jnp.int32, (q_rows, 128), 0) // q_len
            == lax.broadcasted_iota(jnp.int32, (q_rows, 128), 1)).astype(jnp.bfloat16)
 
-    def scores(slot, rows):
+    def scores(slots, rows):
         best = jnp.concatenate(rows, axis=0)
         hi = best.astype(jnp.bfloat16)
         r1 = best - hi.astype(jnp.float32)
         mid = r1.astype(jnp.bfloat16)
         lo = (r1 - mid.astype(jnp.float32)).astype(jnp.bfloat16)
-        s = jnp.dot(hi, sel, preferred_element_type=jnp.float32)
-        s = s + (jnp.dot(mid, sel, preferred_element_type=jnp.float32)
-                 + jnp.dot(lo, sel, preferred_element_type=jnp.float32))
-        return pltpu.roll(s, slot * pairs, 1)
+        s = jnp.dot(jnp.concatenate([hi, mid, lo], axis=0), sel, preferred_element_type=jnp.float32)
+        m = best.shape[0]
+        s = s[:m] + (s[m:2 * m] + s[2 * m:])
+        return functools.reduce(lambda x, y: x + y, [
+            pltpu.roll(s[i * pairs:(i + 1) * pairs], slot * pairs, 1) for i, slot in enumerate(slots)])
 
     rows = []
     for g in range(n_gran):
@@ -120,7 +121,7 @@
         else:
             rows += [best_of(me, (g - 1) * gran + k) for k in range(gran)]
     rows += [best_of(me, (n_gran - 1) * gran + k) for k in range(gran)]
-    total = scores(me, rows)
+    total = scores([me], rows)
 
     def forward(h, i):
         slot = dev(h, False)
@@ -128,8 +129,7 @@
         sends.append(send(slot, partner, i))
 
     def blocks(slots):
-        return functools.reduce(lambda x, y: x + y, [
-            scores(slot, [best_of(slot, j) for j in range(pairs)]) for slot in slots])
+        return scores(slots, [best_of(slot, j) for slot in slots for j in range(pairs)])
 
     for i, h in enumerate(hops[:2]):
         forward(h, len(hops) + 1 + i)
@@ -147,7 +147,7 @@
     mine = pl.ds(pl.multiple_of(me * pairs, pairs), pairs)
     s_all[mine, :] = total
     s_sends = []
-    for o in range(1, n):
+    for o in sorted(range(1, n), key=lambda o: -min(o, n - o)):
         c = pltpu.make_async_remote_copy(
             src_ref=s_all.at[mine], dst_ref=s_all.at[mine], send_sem=s_send.at[o], recv_sem=s_recv.at[me],
             device_id={'data': lax.rem(me + o, n)}, device_id_type=MESH)

time: 41.1 us -> 40 us (0.973)
  Pallas kernels: 39.5 us -> 38.5 us
    pallas_call x1, Pallas kernels: 37.9 us -> 36.8 us  [local_loss(): pl.pallas_call(functools.partial(kernel, (n, pairs, q_len, d_len, gran)),...]
where the time goes in v4:
time: 40 us; the launch traced here: 39.9 us
  Pallas kernels  38.5 us (96%)
  between operations  1.45 us (4%)
    pallas_call x1, Pallas kernels, local_loss(): pl.pallas_call(functools.partial(kernel, (n, pairs, q_len, d_len, gran)),...  36.8 us
    pallas_call x1, Pallas kernels, local_loss(): pl.pallas_call(functools.partial(losses, pairs), out_shape=(jax.ShapeDtyp...  1.63 us

profile of v4, /device:TPU:113, one launch (start us, length us, event | category | flops | bytes accessed | tf_op | source)
XLA Modules:
  0.0 39.9 jit_solution(9630761614842606910)
XLA Ops:
  1.3 36.8 %shard_map.85.s_ref = f32[128,128]{1,0:T(8,128)} custom-call(bf16[512,1024]{1,0:T(8,128)(2,1)} %bitcast.7, bf16[8192,1024]{1,0:T(8,128)(2,1)} %bitcast.6, bf16[1024,128]{1,0:T(8,128)(2,1)} %w_hbm.1, s32[16,32]{1,0:T(8,128)} %qm_hbm.1, s32[16,512]{1,0:T(8,128)} %dm_hbm.1), custom_call_target="tpu_custom_call" | custom-call | tf_op jit(solution)/shard_map/pallas_call | solution.py:198
  38.1 1.6 %shard_map.86 = (f32[1,16]{1,0:T(1,128)}, f32[1,16]{1,0:T(1,128)}, f32[1]{0:T(128)}) custom-call(f32[128,128]{1,0:T(8,128)} %shard_map.85.s_ref, f32[1]{0:T(128)} %bitcast.5.temp_ref), custom_call_target="tpu_custom_call" | custom-call | tf_op jit(solution)/shard_map/pallas_call | solution.py:223

commit v5 on v4

--- a/solution.py
+++ b/solution.py
@@ -7,6 +7,7 @@
 from jax.sharding import PartitionSpec as P
 
 MESH = pl.DeviceIdType.MESH
+SCOPED = 60 * 1024 * 1024
 
 
 def unit_rows(x):
@@ -197,7 +198,7 @@
         vmem, smem = pl.BlockSpec(memory_space=pltpu.VMEM), pl.BlockSpec(memory_space=pltpu.SMEM)
         scores = pl.pallas_call(
             functools.partial(kernel, (n, pairs, q_len, d_len, gran)),
-            out_shape=jax.ShapeDtypeStruct((n * pairs, n * pairs), jnp.float32),
+            out_shape=pltpu.VMEM((n * pairs, n * pairs), jnp.float32),
             in_specs=[hbm] * 5,
             out_specs=vmem,
             scratch_shapes=[
@@ -217,7 +218,7 @@
                 pltpu.SemaphoreType.DMA((n,)),
             ],
             compiler_params=pltpu.CompilerParams(
-                collective_id=0, has_side_effects=True),
+                collective_id=0, has_side_effects=True, vmem_limit_bytes=SCOPED - 80 * 1024),
         )(q_hidden.reshape(pairs * q_len, hidden), d_hidden.reshape(pairs * d_len, hidden), w_proj,
           q_mask, d_mask)
         lq, ld, lm = pl.pallas_call(
@@ -226,6 +227,7 @@
                        jax.ShapeDtypeStruct((1,), jnp.float32)),
             in_specs=[vmem, smem],
             out_specs=(vmem, vmem, smem),
+            compiler_params=pltpu.CompilerParams(vmem_limit_bytes=4 * 1024 * 1024),
         )(scores, temperature.reshape(1))
         return lq.reshape(pairs), ld.reshape(pairs), lm
 

time: 40 us -> 38.5 us (0.963)
  Pallas kernels: 38.5 us -> 37 us
    pallas_call x1, Pallas kernels: 1.63 us -> 0.79 us  [local_loss(): pl.pallas_call(functools.partial(losses, pairs), out_shape=(jax.ShapeDtyp...]
    pallas_call x1, Pallas kernels: 36.8 us -> 36.2 us  [local_loss(): pl.pallas_call(functools.partial(kernel, (n, pairs, q_len, d_len, gran)),...]
where the time goes in v5:
time: 38.5 us; the launch traced here: 38.4 us
  Pallas kernels  37 us (96%)
  between operations  1.45 us (4%)
    pallas_call x1, Pallas kernels, local_loss(): pl.pallas_call(functools.partial(kernel, (n, pairs, q_len, d_len, gran)),...  36.2 us
    pallas_call x1, Pallas kernels, local_loss(): pl.pallas_call(functools.partial(losses, pairs), out_shape=(jax.ShapeDtyp...  0.79 us

profile of v5, /device:TPU:113, one launch (start us, length us, event | category | flops | bytes accessed | tf_op | source)
XLA Modules:
  0.0 38.4 jit_solution(13002803749098852394)
XLA Ops:
  1.3 36.2 %shard_map.85.s_ref = f32[128,128]{1,0:T(8,128)S(1)} custom-call(bf16[512,1024]{1,0:T(8,128)(2,1)} %bitcast.7, bf16[8192,1024]{1,0:T(8,128)(2,1)} %bitcast.6, bf16[1024,128]{1,0:T(8,128)(2,1)} %w_hbm.1, s32[16,32]{1,0:T(8,128)} %qm_hbm.1, s32[16,512]{1,0:T(8,128)} %dm_hbm.1), custom_call_target="tpu_custom_call" | custom-call | tf_op jit(solution)/shard_map/pallas_call | solution.py:199
  37.5 0.8 %shard_map.86 = (f32[1,16]{1,0:T(1,128)}, f32[1,16]{1,0:T(1,128)}, f32[1]{0:T(128)}) custom-call(f32[128,128]{1,0:T(8,128)S(1)} %shard_map.85.s_ref, f32[1]{0:T(128)} %bitcast.5.temp_ref), custom_call_target="tpu_custom_call" | custom-call | tf_op jit(solution)/shard_map/pallas_call | solution.py:224

commit v6 on v5

--- a/solution.py
+++ b/solution.py
@@ -39,8 +39,7 @@
     for g in range(n_gran):
         c = pltpu.make_async_copy(d_hbm.at[pl.ds(g * grows, grows)], dh.at[pl.ds(g * grows, grows)], d_sem.at[g])
         d_copies.append(c)
-    for c in d_copies[:2]:
-        c.start()
+    d_copies[0].start()
 
     barrier = pltpu.get_barrier_semaphore()
     for o in range(1, n):
@@ -55,6 +54,7 @@
 
     for c in ins[2:]:
         c.wait()
+    d_copies[1].start()
 
     def send(slot, target, i):
         c = pltpu.make_async_remote_copy(
@@ -82,10 +82,11 @@
         qall[me] = jnp.where(q_keep > 0.5, xq, 0.0).T.astype(jnp.bfloat16)
 
     def project(g):
-        here = pl.ds(g * grows, grows)
-        x = jnp.dot(dh[here, :], w[...], preferred_element_type=jnp.float32)
-        r = lax.rsqrt(jnp.sum(x * x, axis=1, keepdims=True))
-        u[here, :] = (x * jnp.where(bias[here, :] == 0.0, r, 0.0)).astype(jnp.bfloat16)
+        for k in range(gran):
+            here = pl.ds(g * grows + k * d_len, d_len)
+            x = jnp.dot(dh[here, :], w[...], preferred_element_type=jnp.float32)
+            r = lax.rsqrt(jnp.sum(x * x, axis=1, keepdims=True))
+            u[here, :] = (x * jnp.where(bias[here, :] == 0.0, r, 0.0)).astype(jnp.bfloat16)
 
     def best_of(slot, j):
         here = pl.ds(j * d_len, d_len)

time: 38.5 us -> 36.5 us (0.948)
  Pallas kernels: 37 us -> 35 us
    pallas_call x1, Pallas kernels: 36.2 us -> 34.2 us  [local_loss(): pl.pallas_call(functools.partial(kernel, (n, pairs, q_len, d_len, gran)),...]
where the time goes in v6:
time: 36.5 us; the launch traced here: 36.4 us
  Pallas kernels  35 us (96%)
  between operations  1.45 us (4%)
    pallas_call x1, Pallas kernels, local_loss(): pl.pallas_call(functools.partial(kernel, (n, pairs, q_len, d_len, gran)),...  34.2 us
    pallas_call x1, Pallas kernels, local_loss(): pl.pallas_call(functools.partial(losses, pairs), out_shape=(jax.ShapeDtyp...  0.79 us

profile of v6, /device:TPU:113, one launch (start us, length us, event | category | flops | bytes accessed | tf_op | source)
XLA Modules:
  0.0 36.4 jit_solution(4927398681286520011)
XLA Ops:
  1.3 34.2 %shard_map.85.s_ref = f32[128,128]{1,0:T(8,128)S(1)} custom-call(bf16[512,1024]{1,0:T(8,128)(2,1)} %bitcast.7, bf16[8192,1024]{1,0:T(8,128)(2,1)} %bitcast.6, bf16[1024,128]{1,0:T(8,128)(2,1)} %w_hbm.1, s32[16,32]{1,0:T(8,128)} %qm_hbm.1, s32[16,512]{1,0:T(8,128)} %dm_hbm.1), custom_call_target="tpu_custom_call" | custom-call | tf_op jit(solution)/shard_map/pallas_call | solution.py:200
  35.4 0.8 %shard_map.86 = (f32[1,16]{1,0:T(1,128)}, f32[1,16]{1,0:T(1,128)}, f32[1]{0:T(128)}) custom-call(f32[128,128]{1,0:T(8,128)S(1)} %shard_map.85.s_ref, f32[1]{0:T(128)} %bitcast.5.temp_ref), custom_call_target="tpu_custom_call" | custom-call | tf_op jit(solution)/shard_map/pallas_call | solution.py:225
